TPU v7x, 256 devices: a whole 4x4x8 slice. The times are simulated.
256 devices in a mesh: gx: 16 (over z, core), gy: 4 (over y), gz: 4 (over x).
Axes of the slice: x: 4, y: 4, z: 8, core: 2. Of those that a mesh axis runs over, the one named last changes fastest.
Arguments:
- images: bfloat16 [256, 5, 524288], P(('gx', 'gy', 'gz')), may hold values from 0 to 0.015625
- order: int32 [256], replicated, may hold values from 0 to 255, as said below
Outputs:
- frame: float32 [5, 524288], P(None, 'gx')
Inputs may be any that keep to these rules, and one draw needn't show every extreme that they name: order is a permutation of the bricks, where brick r sits at index r // 16 along gx, (r // 4) % 4 along gy and r % 4 along gz; the bricks of one gz index take consecutive places, within them the bricks of one (gy, gz) pair take consecutive places; the order of gz indices, the order of gy indices within each gz index and the order of gx indices within each (gy, gz) pair are arbitrary and may differ from slab to slab and from column to column.
All inputs are finite; a program needn't handle non-finite values.
Results may differ from a plain program's by a relative error of at most 0.0003.
Values may be sent and summed in bfloat16 or wider, within the bound.
No kernel may reach another device: no remote copies, remote signals or barrier semaphores. Data moves between devices by JAX's collectives and lax.ppermute only.
A program may use at most 64 MiB of HBM per device.

v0:
```python
import jax
import jax.numpy as jnp
from jax import lax
from jax.sharding import PartitionSpec as P


def exchange_in_groups(array, axis, split_dim, concat_dim, work, item_dim, out_dim):

    def moved(group):
        return lax.all_to_all(group, axis, split_axis=split_dim, concat_axis=concat_dim, tiled=True)

    items = jax.tree.leaves(array)[0].shape[item_dim]
    ends = [items * k // 2 for k in range(2 + 1)] if items % 2 == 0 else [0, items]
    groups = [
        jax.tree.map(lambda a: lax.slice_in_dim(a, low, high, axis=item_dim), array)
        for low, high in zip(ends, ends[1:])
    ]
    arrived = [moved(group) for group in groups]
    made = [work(group) for group in arrived]
    return jax.tree.map(lambda *parts: jnp.concatenate(parts, axis=out_dim), *made)


def composite(stacked, member_keys):
    ranked = jnp.argsort(member_keys)

    def layer(total, member):
        picture = lax.dynamic_index_in_dim(stacked, member, 0, keepdims=False).astype(jnp.float32)
        return (total + (1.0 - total[4:5]) * picture, None)

    start = jnp.zeros(stacked.shape[1:], jnp.float32)
    total, _ = lax.scan(layer, start, ranked)
    return total[None]


def per_device(images, order):
    count_x = lax.axis_size("gx")
    count_y = lax.axis_size("gy")
    count_z = lax.axis_size("gz")
    bricks_all = count_x * count_y * count_z
    place_y = lax.axis_index("gy")
    place_z = lax.axis_index("gz")
    grid_order = order.reshape(count_x, count_y, count_z)
    column_order = lax.dynamic_index_in_dim(grid_order, place_z, 2, keepdims=False)
    pixels = images.shape[2]
    layers = images.reshape(1, images.shape[1], bricks_all, pixels // bricks_all)
    first_keys = lax.dynamic_index_in_dim(column_order, place_y, 1, keepdims=False)
    second_keys = jnp.min(column_order, axis=0)

    def first_blend(stacked):
        return composite(stacked, first_keys)

    partial_value = exchange_in_groups(layers, "gx", 2, 0, first_blend, 3, 3)
    partial_value = composite(
        lax.all_to_all(partial_value, "gy", split_axis=2, concat_axis=0, tiled=True), second_keys
    )
    slab_keys = jnp.min(grid_order, axis=(0, 1))
    stacked = lax.all_gather(partial_value, "gz", axis=0, tiled=True)
    partial_value = composite(stacked, slab_keys)
    tiles = lax.all_gather(partial_value, "gy", axis=2, tiled=True)
    return tiles.reshape(tiles.shape[1], -1)


def solution(mesh):
    in_specs = (P(("gx", "gy", "gz"), None, None), P())
    out_specs = P(None, "gx")
    return jax.shard_map(
        per_device, mesh=mesh, in_specs=in_specs, out_specs=out_specs, check_vma=False
    )
```

profile of v0, /device:TPU:34, one launch (start us, length us, event | category | flops | bytes accessed | tf_op | source)
XLA Modules:
  0.0 323.7 jit_solution(4694022035820892433)
XLA Ops:
  0.0 5.9 %fusion.8 = (bf16[1,5,256,1024]{3,1,0,2:T(8,128)(2,1)}, bf16[1,5,256,1024]{3,1,0,2:T(8,128)(2,1)}) fusion(bf16[1,5,256,2048]{3,1,0,2:T(8,128)(2,1)} %bitcast.71), kind=kLoop, calls=%fused_computation.24 | loop fusion | bytes 10485760 | tf_op jit(solution)/shard_map/slice | solution.py:15
  5.9 8.7 %all-to-all-start.1 = ((bf16[1,5,256,1024]{3,1,0,2:T(8,128)(2,1)}), bf16[1,5,256,1024]{3,1,0,2:T(8,128)(2,1)}, u32[]{:S(2)}, u32[]{:S(2)}) async-start(bf16[1,5,256,1024]{3,1,0,2:T(8,128)(2,1)} %get-tuple-element.256), calls=%async_computation.1 | async-start | bytes 8388608 | tf_op jit(solution)/shard_map/all_to_all | solution.py:10
  15.2 1.3 sort.52
  16.6 90.3 %all-to-all-done.1 = bf16[1,5,256,1024]{3,1,0,2:T(8,128)(2,1)} async-done(((bf16[1,5,256,1024]{3,1,0,2:T(8,128)(2,1)}), bf16[1,5,256,1024]{3,1,0,2:T(8,128)(2,1)}, u32[]{:S(2)}, u32[]{:S(2)}) %all-to-all-start.1) | async-done | bytes 2621472 | tf_op jit(solution)/shard_map/all_to_all | solution.py:10
  106.9 6.7 %all-to-all-start = ((bf16[1,5,256,1024]{3,1,0,2:T(8,128)(2,1)}), bf16[1,5,256,1024]{3,1,0,2:T(8,128)(2,1)}, u32[]{:S(2)}, u32[]{:S(2)}) async-start(bf16[1,5,256,1024]{3,1,0,2:T(8,128)(2,1)} %get-tuple-element.255), calls=%async_computation | async-start | bytes 8388608 | tf_op jit(solution)/shard_map/all_to_all | solution.py:10
  113.7 4.1 %copy.30 = bf16[16,5,16,1024]{3,2,1,0:T(8,128)(2,1)S(1)} copy(bf16[16,5,16,1024]{3,1,2,0:T(8,128)(2,1)} %bitcast.9) | data formatting | bytes 5242880
  117.8 39.5 %while.45 = (s32[]{:T(128)}, f32[5,16,1024]{2,1,0:T(8,128)S(1)}, s32[16]{0:T(128)S(1)}, bf16[16,5,16,1024]{3,2,1,0:T(8,128)(2,1)S(1)}, s32[]{:T(128)}, /*index=5*/s32[]{:T(128)}, s32[]{:T(128)}) while((s32[]{:T(128)}, f32[5,16,1024]{2,1,0:T(8,128)S(1)}, s32[16]{0:T(128)S(1)}, bf16[16,5,16,1024]{3,2,1,0:T(8,128)(2,1)S(1)}, ...), condition=%wide.region_8.9_spmd.clone, body=%wide.region_7.8_spmd.clone.sunk | while | flops 425990 | bytes 1671306 | solution.py:31
  157.3 48.7 %all-to-all-done = bf16[1,5,256,1024]{3,1,0,2:T(8,128)(2,1)} async-done(((bf16[1,5,256,1024]{3,1,0,2:T(8,128)(2,1)}), bf16[1,5,256,1024]{3,1,0,2:T(8,128)(2,1)}, u32[]{:S(2)}, u32[]{:S(2)}) %all-to-all-start) | async-done | bytes 2621472 | tf_op jit(solution)/shard_map/all_to_all | solution.py:10
  205.9 4.1 %copy.28 = bf16[16,5,16,1024]{3,2,1,0:T(8,128)(2,1)S(1)} copy(bf16[16,5,16,1024]{3,1,2,0:T(8,128)(2,1)} %bitcast.4) | data formatting | bytes 5242880
  210.1 43.6 %while.44 = (s32[]{:T(128)}, f32[5,16,1024]{2,1,0:T(8,128)S(1)}, s32[16]{0:T(128)S(1)}, bf16[16,5,16,1024]{3,2,1,0:T(8,128)(2,1)S(1)}, s32[]{:T(128)}, /*index=5*/s32[]{:T(128)}, s32[]{:T(128)}) while((s32[]{:T(128)}, f32[5,16,1024]{2,1,0:T(8,128)S(1)}, s32[16]{0:T(128)S(1)}, bf16[16,5,16,1024]{3,2,1,0:T(8,128)(2,1)S(1)}, ...), condition=%wide.region_6.7_spmd.clone, body=%wide.region_5.6_spmd.clone.sunk | while | flops 425990 | bytes 1671306 | solution.py:31
  210.1 0.6 dynamic_slice.61
  212.8 0.6 dynamic_slice.61
  215.5 0.6 dynamic_slice.61
  218.3 0.6 dynamic_slice.61
  253.8 1.5 copy.31
  255.3 4.5 %all-to-all-start.2 = ((f32[1,5,16,2048]{3,0,1,2:T(1,128)}), f32[1,5,16,2048]{3,0,1,2:T(1,128)S(1)}, u32[]{:S(2)}, u32[]{:S(2)}) async-start(f32[1,5,16,2048]{3,0,1,2:T(1,128)} %copy.31), calls=%async_computation.2 | async-start | bytes 1310720 | tf_op jit(solution)/shard_map/all_to_all | solution.py:54
  260.0 0.8 sort.51
  260.8 0.8 sort.50
  261.5 9.6 %all-to-all-done.2 = f32[1,5,16,2048]{3,0,1,2:T(1,128)S(1)} async-done(((f32[1,5,16,2048]{3,0,1,2:T(1,128)}), f32[1,5,16,2048]{3,0,1,2:T(1,128)S(1)}, u32[]{:S(2)}, u32[]{:S(2)}) %all-to-all-start.2) | async-done | bytes 655392 | tf_op jit(solution)/shard_map/all_to_all | solution.py:54
  271.5 11.0 %while.46 = (s32[]{:T(128)}, f32[5,4,2048]{2,1,0:T(4,128)S(1)}, s32[4]{0:T(128)S(1)}, f32[4,5,4,2048]{3,2,1,0:T(4,128)S(1)}, s32[]{:T(128)}, /*index=5*/s32[]{:T(128)}, s32[]{:T(128)}) while((s32[]{:T(128)}, f32[5,4,2048]{2,1,0:T(4,128)S(1)}, s32[4]{0:T(128)S(1)}, f32[4,5,4,2048]{3,2,1,0:T(4,128)S(1)}, s32[]{:T(128)}, ...), condition=%wide.region_10.11_spmd.clone, body=%wide.region_9.10_spmd.clone.sunk | while | flops 172038 | bytes 917642 | solution.py:31
  282.5 14.0 %all-gather = f32[20,4,2048]{2,1,0:T(4,128)S(1)} all-gather(f32[5,4,2048]{2,1,0:T(4,128)S(1)} %get-tuple-element.101), channel_id=2, replica_groups=mesh['gx'=16,'gy'=4,'gz'=4] {'gz'}, dimensions={0}, use_global_device_ids=true | all-gather | bytes 819200 | tf_op jit(solution)/shard_map/all_gather | solution.py:57
  296.4 10.9 %while.47 = (s32[]{:T(128)}, f32[5,4,2048]{2,1,0:T(4,128)S(1)}, s32[4]{0:T(128)S(1)}, f32[4,5,4,2048]{3,2,1,0:T(4,128)S(1)}, s32[]{:T(128)}, /*index=5*/s32[]{:T(128)}, s32[]{:T(128)}) while((s32[]{:T(128)}, f32[5,4,2048]{2,1,0:T(4,128)S(1)}, s32[4]{0:T(128)S(1)}, f32[4,5,4,2048]{3,2,1,0:T(4,128)S(1)}, s32[]{:T(128)}, ...), condition=%wide.region_12.13_spmd.clone, body=%wide.region_11.12_spmd.clone.sunk | while | flops 172038 | bytes 917642 | solution.py:31
  307.5 15.2 %all-gather.1 = f32[5,16,2048]{2,0,1:T(8,128)S(1)} all-gather(f32[5,4,2048]{2,0,1:T(8,128)S(1)} %copy.34), channel_id=3, replica_groups=mesh['gx'=16,'gy'=4,'gz'=4] {'gy'}, dimensions={1}, use_global_device_ids=true | all-gather | bytes 819200 | tf_op jit(solution)/shard_map/all_gather | solution.py:59
  322.7 1.0 copy.65
  (173 shorter events, 28.2 us)
Async XLA Ops:
  5.9 8.7 %copy-start = (s32[256]{0:T(256)S(1)}, s32[256]{0:T(256)}, u32[]{:S(2)}) copy-start(s32[256]{0:T(256)} %param.11) | copy-start | bytes 3076
  5.9 101.0 %all-to-all-start.1 = ((bf16[1,5,256,1024]{3,1,0,2:T(8,128)(2,1)}), bf16[1,5,256,1024]{3,1,0,2:T(8,128)(2,1)}, u32[]{:S(2)}, u32[]{:S(2)}) async-start(bf16[1,5,256,1024]{3,1,0,2:T(8,128)(2,1)} %get-tuple-element.256), calls=%async_computation.1 | async-start | bytes 8388608 | tf_op jit(solution)/shard_map/all_to_all | solution.py:10
  106.9 99.0 %all-to-all-start = ((bf16[1,5,256,1024]{3,1,0,2:T(8,128)(2,1)}), bf16[1,5,256,1024]{3,1,0,2:T(8,128)(2,1)}, u32[]{:S(2)}, u32[]{:S(2)}) async-start(bf16[1,5,256,1024]{3,1,0,2:T(8,128)(2,1)} %get-tuple-element.255), calls=%async_computation | async-start | bytes 8388608 | tf_op jit(solution)/shard_map/all_to_all | solution.py:10
  255.3 15.9 %all-to-all-start.2 = ((f32[1,5,16,2048]{3,0,1,2:T(1,128)}), f32[1,5,16,2048]{3,0,1,2:T(1,128)S(1)}, u32[]{:S(2)}, u32[]{:S(2)}) async-start(f32[1,5,16,2048]{3,0,1,2:T(1,128)} %copy.31), calls=%async_computation.2 | async-start | bytes 1310720 | tf_op jit(solution)/shard_map/all_to_all | solution.py:54
where the time goes:
time: 325 us; the launch traced here: 324 us
  waiting for transfers between devices  149 us (46%)
  loops' own time  75.7 us (23%)
  local copies, waits for them, and re-layouts  40.7 us (13%)
  blocking collectives  29.2 us (9%)
  starting transfers between devices  19.9 us (6%)
  other arithmetic  9.4 us (3%)
    all_to_all x2, waiting for transfers between devices, moved(): lax.all_to_all(group, axis, split_axis=split_dim, concat_axis=concat_dim,...  139 us
    another operation x4, loops' own time, composite(): total, _ = lax.scan(layer, start, ranked)  75.7 us
    dynamic_slice x40, local copies, waits for them, and re-layouts, composite(): total, _ = lax.scan(layer, start, ranked)  23 us
    all_to_all x2, starting transfers between devices, moved(): lax.all_to_all(group, axis, split_axis=split_dim, concat_axis=concat_dim,...  15.5 us
    all_gather x1, blocking collectives, per_device(): tiles = lax.all_gather(partial_value, 'gy', axis=2, tiled=True)  15.2 us
    all_gather x1, blocking collectives, per_device(): stacked = lax.all_gather(partial_value, 'gz', axis=0, tiled=True)  14 us
    all_to_all x1, waiting for transfers between devices, per_device(): lax.all_to_all(partial_value, 'gy', split_axis=2, concat_axis=0, tiled=True)  9.64 us
    unnamed x6, local copies, waits for them, and re-layouts  9.53 us
  transfers between devices with their start and end apart: 3, of which 3 were waited for; matrix products, arithmetic and copies ran while one was open for 6% of the time, Pallas kernels for 0%

commit v1 on v0

v1 whole, which is shorter than its diff:
```python
import jax
import jax.numpy as jnp
from jax import lax
from jax.experimental import pallas as pl
from jax.experimental.pallas import tpu as pltpu
from jax.sharding import PartitionSpec as P


DEPTH_RANGE = 4.02
STEPS = 65535.0 / DEPTH_RANGE


def opacity_kernel(images, out):
    rows, lanes = out.shape[1:]
    for p in range(out.shape[0]):
        out[p] = images[0, images.shape[1] - 1, p * rows * lanes : (p + 1) * rows * lanes].reshape(rows, lanes)


def opacity_tiles(images, count, rows, lanes):
    step = 64
    return pl.pallas_call(
        opacity_kernel,
        grid=(count // step,),
        in_specs=[pl.BlockSpec((1, images.shape[1], step * rows * lanes), lambda i: (0, 0, i))],
        out_specs=pl.BlockSpec((step, rows, lanes), lambda i: (i, 0, 0)),
        out_shape=jax.ShapeDtypeStruct((count, rows, lanes), images.dtype),
        compiler_params=pltpu.CompilerParams(vmem_limit_bytes=16 << 20),
        cost_estimate=pl.CostEstimate(flops=images.size, bytes_accessed=2 * images.size, transcendentals=0),
        name="opacity_tiles",
    )(images)


def front_kernel(brick, opacity, codes, total):
    count = opacity.shape[0]

    def place(p, done):
        r = brick[p]
        left = 1.0 - done
        code = jnp.floor(jnp.log(left) * -STEPS + 0.5).astype(jnp.int32) - 32768
        codes[r] = code.astype(jnp.int16)
        return done + left * opacity[r].astype(jnp.float32)

    total[...] = lax.fori_loop(0, count, place, jnp.zeros(total.shape, jnp.float32), unroll=8)


def front(brick, opacity):
    count, rows, lanes = opacity.shape
    return pl.pallas_call(
        front_kernel,
        in_specs=[
            pl.BlockSpec(memory_space=pltpu.SMEM),
            pl.BlockSpec(memory_space=pltpu.VMEM),
        ],
        out_specs=[
            pl.BlockSpec(memory_space=pltpu.VMEM),
            pl.BlockSpec(memory_space=pltpu.VMEM),
        ],
        out_shape=[
            jax.ShapeDtypeStruct((count, rows, lanes), jnp.int16),
            jax.ShapeDtypeStruct((rows, lanes), jnp.float32),
        ],
        cost_estimate=pl.CostEstimate(flops=8 * opacity.size, bytes_accessed=4 * opacity.size, transcendentals=opacity.size),
        compiler_params=pltpu.CompilerParams(vmem_limit_bytes=16 << 20),
        name="front",
    )(brick, opacity)


def blend_kernel(member, codes, *refs):
    pictures, out = refs[:-1], refs[-1]
    for g in range(out.shape[0]):
        sums = [jnp.zeros(out.shape[2:], jnp.float32) for _ in range(out.shape[1])]
        for j, picture in enumerate(pictures):
            code = codes[g, member[j]].astype(jnp.int32).astype(jnp.float32)
            left = jnp.exp((code + 32768.0) * (-1.0 / STEPS))
            for c in range(out.shape[1]):
                sums[c] = sums[c] + left * picture[c, g].astype(jnp.float32)
        for c in range(out.shape[1]):
            out[g, c] = sums[c]


def blend(member, codes, pictures, step=4):
    bands, members, rows, lanes = codes.shape
    colours = pictures[0].shape[0]
    return pl.pallas_call(
        blend_kernel,
        grid_spec=pltpu.PrefetchScalarGridSpec(
            num_scalar_prefetch=1,
            grid=(bands // step,),
            in_specs=[pl.BlockSpec((step, members, rows, lanes), lambda i, m: (i, 0, 0, 0))]
            + [pl.BlockSpec((colours, step, rows, lanes), lambda i, m: (0, i, 0, 0)) for _ in pictures],
            out_specs=pl.BlockSpec((step, colours, rows, lanes), lambda i, m: (i, 0, 0, 0)),
        ),
        out_shape=jax.ShapeDtypeStruct((bands, colours, rows, lanes), jnp.float32),
        cost_estimate=pl.CostEstimate(
            flops=2 * colours * codes.size, bytes_accessed=2 * (colours + 1) * codes.size, transcendentals=codes.size
        ),
        compiler_params=pltpu.CompilerParams(vmem_limit_bytes=24 << 20),
        name="blend",
    )(member, codes, *pictures)


def per_device(images, order):
    count_x = lax.axis_size("gx")
    count_y = lax.axis_size("gy")
    count_z = lax.axis_size("gz")
    plane = count_y * count_z
    bricks = count_x * plane
    channels, pixels = images.shape[1:]
    colours = channels - 1
    lanes = 128
    rows = pixels // (bricks * lanes)
    place_y = lax.axis_index("gy")
    place_z = lax.axis_index("gz")

    opacity = opacity_tiles(images, bricks, rows, lanes)
    opacity = lax.all_to_all(opacity, ("gx", "gy", "gz"), 0, 0, tiled=True)

    places = jnp.arange(bricks, dtype=jnp.int32)
    brick = jnp.sum(jnp.where(order[None, :] == places[:, None], places[None, :], 0), axis=1, dtype=jnp.int32)

    colour_tiles = images[0, :colours].reshape(colours, count_x, plane, rows, lanes)
    pictures, member = [], []
    for dy in range(count_y):
        for dz in range(count_z):
            target = ((place_y + dy) % count_y) * count_z + (place_z + dz) % count_z
            piece = lax.dynamic_index_in_dim(colour_tiles, target, 2, keepdims=False)
            if dy or dz:
                moves = [
                    (a * count_z + b, ((a + dy) % count_y) * count_z + (b + dz) % count_z)
                    for a in range(count_y)
                    for b in range(count_z)
                ]
                piece = lax.ppermute(piece, ("gy", "gz"), moves)
            pictures.append(piece)
            member.append(((place_y - dy) % count_y) * count_z + (place_z - dz) % count_z)
    member = jnp.stack(member).astype(jnp.int32)

    codes, total = front(brick, opacity)
    codes = lax.all_to_all(codes, "gx", 0, 0, tiled=True).reshape(count_x, plane, rows, lanes)
    part = blend(member, codes, pictures)
    part = lax.all_to_all(part, "gx", 0, 0, tiled=True)
    piece = jnp.concatenate([jnp.sum(part, axis=0), total[None]], axis=0)
    piece = piece.reshape(channels, 1, rows * lanes)
    band = lax.all_to_all(jnp.broadcast_to(piece, (channels, plane, rows * lanes)), ("gy", "gz"), 1, 1, tiled=True)
    return band.reshape(channels, -1)


def solution(mesh):
    in_specs = (P(("gx", "gy", "gz"), None, None), P())
    out_specs = P(None, "gx")

    return jax.shard_map(per_device, mesh=mesh, in_specs=in_specs, out_specs=out_specs, check_vma=False)
```

time: 325 us -> 208 us (0.64)
  the two profiles are of different devices: /device:TPU:34 before, /device:TPU:1 now
where the time goes in v1:
time: 208 us; the launch traced here: 207 us
  starting transfers between devices  69.6 us (33%)
  blocking collectives  55.9 us (27%)
  waiting for transfers between devices  53.4 us (26%)
  local copies, waits for them, and re-layouts  18.9 us (9%)
  Pallas kernels  8.95 us (4%)
    ppermute x15, starting transfers between devices, per_device(): piece = lax.ppermute(piece, ('gy', 'gz'), moves)  48.7 us
    all_to_all x1, blocking collectives, per_device(): part = lax.all_to_all(part, 'gx', 0, 0, tiled=True)  35.8 us
    all_to_all x1, waiting for transfers between devices, per_device(): opacity = lax.all_to_all(opacity, ('gx', 'gy', 'gz'), 0, 0, tiled=True)  29.8 us
    ppermute x15, waiting for transfers between devices, per_device(): piece = lax.ppermute(piece, ('gy', 'gz'), moves)  23.7 us
    all_to_all x1, blocking collectives, per_device(): lax.all_to_all(jnp.broadcast_to(piece, (channels, plane, rows * lanes)),...  20 us
    all_to_all x1, starting transfers between devices, per_device(): opacity = lax.all_to_all(opacity, ('gx', 'gy', 'gz'), 0, 0, tiled=True)  15.6 us
    unnamed x15, local copies, waits for them, and re-layouts  14.8 us
    all_to_all x1, starting transfers between devices, per_device(): lax.all_to_all(codes, 'gx', 0, 0, tiled=True)  5.26 us
  transfers between devices with their start and end apart: 17, of which 6 were waited for; matrix products, arithmetic and copies ran while one was open for 5% of the time, Pallas kernels for 0%

profile of v1, /device:TPU:1, one launch (start us, length us, event | category | flops | bytes accessed | tf_op | source)
XLA Modules:
  0.0 207.0 jit_solution(12682271468009084024)
XLA Ops:
  0.0 3.4 %copy-done = bf16[1,5,524288]{2,1,0:T(8,128)(2,1)S(1)} copy-done((bf16[1,5,524288]{2,1,0:T(8,128)(2,1)S(1)}, bf16[1,5,524288]{2,1,0:T(8,128)(2,1)}, u32[]{:S(2)}) %copy-start) | copy-done | bytes 5242904
  3.4 2.2 %opacity_tiles.1 = bf16[256,16,128]{2,1,0:T(8,128)(2,1)} custom-call(bf16[1,5,524288]{2,1,0:T(8,128)(2,1)S(1)} %copy-done), custom_call_target="tpu_custom_call" | custom-call | flops 2621440 | bytes 5242880 | tf_op jit(solution)/shard_map/opacity_tiles/pallas_call | solution.py:21
  5.6 15.6 %all-to-all-start = ((bf16[256,16,128]{2,1,0:T(8,128)(2,1)}), bf16[256,16,128]{2,1,0:T(8,128)(2,1)S(1)}, u32[]{:S(2)}, u32[]{:S(2)}) async-start(bf16[256,16,128]{2,1,0:T(8,128)(2,1)} %opacity_tiles.1), calls=%async_computation | async-start | bytes 2097152 | tf_op jit(solution)/shard_map/all_to_all | solution.py:116
  21.4 29.8 %all-to-all-done.opacity = bf16[256,16,128]{2,1,0:T(8,128)(2,1)S(1)} async-done(((bf16[256,16,128]{2,1,0:T(8,128)(2,1)}), bf16[256,16,128]{2,1,0:T(8,128)(2,1)S(1)}, u32[]{:S(2)}, u32[]{:S(2)}) %all-to-all-start) | async-done | bytes 1048608 | tf_op jit(solution)/shard_map/all_to_all | solution.py:116
  51.2 3.0 %front.1 = (s16[256,16,128]{2,1,0:T(8,128)(2,1)}, f32[16,128]{1,0:T(8,128)S(1)}) custom-call(s32[256]{0:T(256)S(1)} %select_reduce_fusion.brick, bf16[256,16,128]{2,1,0:T(8,128)(2,1)S(1)} %all-to-all-done.opacity), custom_call_target="tpu_custom_call" | custom-call | flops 4194304 | bytes 2097152 | tf_op jit(solution)/shard_map/front/pallas_call | solution.py:48
  54.1 5.3 %all-to-all-start.1 = ((s16[256,16,128]{2,1,0:T(8,128)(2,1)}), s16[256,16,128]{2,1,0:T(8,128)(2,1)S(1)}, u32[]{:S(2)}, u32[]{:S(2)}) async-start(s16[256,16,128]{2,1,0:T(8,128)(2,1)} %get-tuple-element.7), calls=%async_computation.1 | async-start | bytes 2097152 | tf_op jit(solution)/shard_map/all_to_all | solution.py:139
  59.4 4.7 %slice_bitcast_fusion = bf16[1,4,4096,128]{3,1,2,0:T(4,128)(2,1)S(1)} fusion(bf16[1,5,524288]{2,1,0:T(8,128)(2,1)} %images.1), kind=kLoop, calls=%fused_computation | loop fusion | bytes 8388608
  64.1 2.5 %copy.70 = bf16[1,4,4096,128]{3,2,1,0:T(8,128)(2,1)} copy(bf16[1,4,4096,128]{3,1,2,0:T(4,128)(2,1)S(1)} %slice_bitcast_fusion) | data formatting | bytes 8388608
  66.6 3.9 %dynamic-slice_bitcast_fusion = (bf16[4,16,16,128]{3,2,1,0:T(8,128)(2,1)S(1)}, bf16[4,16,16,128]{3,2,1,0:T(8,128)(2,1)S(1)}, bf16[4,16,16,128]{3,2,1,0:T(8,128)(...) fusion(bf16[4,16,16,16,128]{4,3,2,1,0:T(8,128)(2,1)} %bitcast.9, ...), kind=kLoop, calls=%fused_computation.1 | loop fusion | bytes 8388672 | tf_op jit(solution)/shard_map/jit(dynamic_index_in_dim)/squeeze | solution.py:126
  71.6 2.3 %collective-permute-start.1 = (bf16[4,16,16,128]{3,2,1,0:T(8,128)(2,1)S(1)}, bf16[4,16,16,128]{3,2,1,0:T(8,128)(2,1)S(1)}, u32[]{:S(2)}, u32[]{:S(2)}) collective-permute-start(bf16[4,16,16,128]{3,2,1,0:T(8,128)(2,1)S(1)} %get-tuple-element.22), channel_id=1, source_target_pairs={{0,2},{1,3},{2,0},{3,1},{4,6},{5,7},{6,4},{7,5},{8,10},{9,11},{10,... | collective-permute-start | bytes 786440 | tf_op jit(solution)/shard_map/ppermute | solution.py:133
  75.2 2.2 %collective-permute-start.11 = (bf16[4,16,16,128]{3,2,1,0:T(8,128)(2,1)S(1)}, bf16[4,16,16,128]{3,2,1,0:T(8,128)(2,1)S(1)}, u32[]{:S(2)}, u32[]{:S(2)}) collective-permute-start(bf16[4,16,16,128]{3,2,1,0:T(8,128)(2,1)S(1)} %get-tuple-element.12), channel_id=1, source_target_pairs={{0,12},{1,13},{2,14},{3,15},{4,0},{5,1},{6,2},{7,3},{8,4},{9,5},{1... | collective-permute-start | bytes 786440 | tf_op jit(solution)/shard_map/ppermute | solution.py:133
  79.6 6.0 %collective-permute-done.1.refs_2_ = bf16[4,16,16,128]{3,2,1,0:T(8,128)(2,1)S(1)} collective-permute-done((bf16[4,16,16,128]{3,2,1,0:T(8,128)(2,1)S(1)}, bf16[4,16,16,128]{3,2,1,0:T(8,128)(2,1)S(1)}, u32[]{:S(2)}, u32[]{:S(2)}) %collective-permute-start.1) | collective-permute-done | bytes 262176 | tf_op jit(solution)/shard_map/ppermute | solution.py:133
  85.6 1.4 collective-permute-done.10.refs_11_
  87.0 4.3 %collective-permute-start.2 = (bf16[4,16,16,128]{3,2,1,0:T(8,128)(2,1)S(1)}, bf16[4,16,16,128]{3,2,1,0:T(8,128)(2,1)S(1)}, u32[]{:S(2)}, u32[]{:S(2)}) collective-permute-start(bf16[4,16,16,128]{3,2,1,0:T(8,128)(2,1)S(1)} %get-tuple-element.21), channel_id=1, source_target_pairs={{0,3},{1,0},{2,1},{3,2},{4,7},{5,4},{6,5},{7,6},{8,11},{9,8},{10,9... | collective-permute-start | bytes 786440 | tf_op jit(solution)/shard_map/ppermute | solution.py:133
  91.3 2.7 %collective-permute-done.11.refs_12_ = bf16[4,16,16,128]{3,2,1,0:T(8,128)(2,1)S(1)} collective-permute-done((bf16[4,16,16,128]{3,2,1,0:T(8,128)(2,1)S(1)}, bf16[4,16,16,128]{3,2,1,0:T(8,128)(2,1)S(1)}, u32[]{:S(2)}, u32[]{:S(2)}) %collective-permute-start.11) | collective-permute-done | bytes 262176 | tf_op jit(solution)/shard_map/ppermute | solution.py:133
  94.0 1.5 collective-permute-start.3
  95.5 11.4 %collective-permute-start.4 = (bf16[4,16,16,128]{3,2,1,0:T(8,128)(2,1)S(1)}, bf16[4,16,16,128]{3,2,1,0:T(8,128)(2,1)S(1)}, u32[]{:S(2)}, u32[]{:S(2)}) collective-permute-start(bf16[4,16,16,128]{3,2,1,0:T(8,128)(2,1)S(1)} %get-tuple-element.19), channel_id=1, source_target_pairs={{0,5},{1,6},{2,7},{3,4},{4,9},{5,10},{6,11},{7,8},{8,13},{9,14},{1... | collective-permute-start | bytes 786440 | tf_op jit(solution)/shard_map/ppermute | solution.py:133
  108.3 2.3 %collective-permute-start.6 = (bf16[4,16,16,128]{3,2,1,0:T(8,128)(2,1)}, bf16[4,16,16,128]{3,2,1,0:T(8,128)(2,1)}, u32[]{:S(2)}, u32[]{:S(2)}) collective-permute-start(bf16[4,16,16,128]{3,2,1,0:T(8,128)(2,1)} %get-tuple-element.17), channel_id=1, source_target_pairs={{0,7},{1,4},{2,5},{3,6},{4,11},{5,8},{6,9},{7,10},{8,15},{9,12},{1... | collective-permute-start | bytes 786440 | tf_op jit(solution)/shard_map/ppermute | solution.py:133
  110.6 1.6 collective-permute-start.7
  112.9 18.2 %collective-permute-start.8 = (bf16[4,16,16,128]{3,2,1,0:T(8,128)(2,1)}, bf16[4,16,16,128]{3,2,1,0:T(8,128)(2,1)}, u32[]{:S(2)}, u32[]{:S(2)}) collective-permute-start(bf16[4,16,16,128]{3,2,1,0:T(8,128)(2,1)} %get-tuple-element.15), channel_id=1, source_target_pairs={{0,9},{1,10},{2,11},{3,8},{4,13},{5,14},{6,15},{7,12},{8,1},{9,2},... | collective-permute-start | bytes 786440 | tf_op jit(solution)/shard_map/ppermute | solution.py:133
  132.0 12.4 %collective-permute-done.7.refs_8_ = bf16[4,16,16,128]{3,2,1,0:T(8,128)(2,1)} collective-permute-done((bf16[4,16,16,128]{3,2,1,0:T(8,128)(2,1)}, bf16[4,16,16,128]{3,2,1,0:T(8,128)(2,1)}, u32[]{:S(2)}, u32[]{:S(2)}) %collective-permute-start.7) | collective-permute-done | bytes 262176 | tf_op jit(solution)/shard_map/ppermute | solution.py:133
  146.2 3.8 %blend.1 = f32[16,4,16,128]{3,2,1,0:T(8,128)S(1)} custom-call(s32[16]{0:T(128)S(1)} %stack.67.member, s16[16,16,16,128]{3,2,1,0:T(8,128)(2,1)S(1)} %bitcast.92, bf16[4,16,16,128]{3,2,1,0:T(8,128)(2,1)S(1)} %get-tuple-element.24.refs_0_, bf16[4,16,16,128]{3,2,1,0:T(8,128)(2,1)S(1)} %collective-permute-done.refs_1_, ...), custom_call_target="tpu_custom_call" | custom-call | flops 4194304 | bytes 5242880 | tf_op jit(solution)/shard_map/blend/pallas_call | solution.py:84
  150.0 35.8 %all_to_all.20 = f32[16,4,16,128]{3,2,1,0:T(8,128)S(1)} all-to-all(f32[16,4,16,128]{3,2,1,0:T(8,128)S(1)} %blend.1), channel_id=1, replica_groups=mesh['gx'=16,'gy'=4,'gz'=4] {'gx'}, dimensions={0} | all-to-all | bytes 1048576 | tf_op jit(solution)/shard_map/all_to_all | solution.py:141
  186.0 20.0 %all_to_all.21 = f32[5,16,2048]{2,0,1:T(8,128)S(1)} all-to-all(f32[5,16,2048]{2,0,1:T(8,128)S(1)} %broadcast_in_dim.26), channel_id=1, replica_groups=mesh['gx'=16,'gy'=4,'gz'=4] {'gy','gz'}, dimensions={1} | all-to-all | bytes 1310720 | tf_op jit(solution)/shard_map/all_to_all | solution.py:144
  (37 shorter events, 10.8 us)
Async XLA Ops:
  0.0 3.4 %copy-start = (bf16[1,5,524288]{2,1,0:T(8,128)(2,1)S(1)}, bf16[1,5,524288]{2,1,0:T(8,128)(2,1)}, u32[]{:S(2)}) copy-start(bf16[1,5,524288]{2,1,0:T(8,128)(2,1)} %images.1) | copy-start | bytes 15728644
  3.4 17.9 %copy-start.5 = (s32[256]{0:T(256)S(1)}, s32[256]{0:T(256)}, u32[]{:S(2)}) copy-start(s32[256]{0:T(256)} %param.3) | copy-start | bytes 3076
  5.6 45.5 %all-to-all-start = ((bf16[256,16,128]{2,1,0:T(8,128)(2,1)}), bf16[256,16,128]{2,1,0:T(8,128)(2,1)S(1)}, u32[]{:S(2)}, u32[]{:S(2)}) async-start(bf16[256,16,128]{2,1,0:T(8,128)(2,1)} %opacity_tiles.1), calls=%async_computation | async-start | bytes 2097152 | tf_op jit(solution)/shard_map/all_to_all | solution.py:116
  54.1 90.2 %all-to-all-start.1 = ((s16[256,16,128]{2,1,0:T(8,128)(2,1)}), s16[256,16,128]{2,1,0:T(8,128)(2,1)S(1)}, u32[]{:S(2)}, u32[]{:S(2)}) async-start(s16[256,16,128]{2,1,0:T(8,128)(2,1)} %get-tuple-element.7), calls=%async_computation.1 | async-start | bytes 2097152 | tf_op jit(solution)/shard_map/all_to_all | solution.py:139
  70.4 8.7 %collective-permute-start = (bf16[4,16,16,128]{3,2,1,0:T(8,128)(2,1)S(1)}, bf16[4,16,16,128]{3,2,1,0:T(8,128)(2,1)S(1)}, u32[]{:S(2)}, u32[]{:S(2)}) collective-permute-start(bf16[4,16,16,128]{3,2,1,0:T(8,128)(2,1)S(1)} %get-tuple-element.23), channel_id=1, source_target_pairs={{0,1},{1,2},{2,3},{3,0},{4,5},{5,6},{6,7},{7,4},{8,9},{9,10},{10,1... | collective-permute-start | bytes 786440 | tf_op jit(solution)/shard_map/ppermute | solution.py:133
  71.6 14.0 %collective-permute-start.1 = (bf16[4,16,16,128]{3,2,1,0:T(8,128)(2,1)S(1)}, bf16[4,16,16,128]{3,2,1,0:T(8,128)(2,1)S(1)}, u32[]{:S(2)}, u32[]{:S(2)}) collective-permute-start(bf16[4,16,16,128]{3,2,1,0:T(8,128)(2,1)S(1)} %get-tuple-element.22), channel_id=1, source_target_pairs={{0,2},{1,3},{2,0},{3,1},{4,6},{5,7},{6,4},{7,5},{8,10},{9,11},{10,... | collective-permute-start | bytes 786440 | tf_op jit(solution)/shard_map/ppermute | solution.py:133
  73.9 13.1 %collective-permute-start.10 = (bf16[4,16,16,128]{3,2,1,0:T(8,128)(2,1)S(1)}, bf16[4,16,16,128]{3,2,1,0:T(8,128)(2,1)S(1)}, u32[]{:S(2)}, u32[]{:S(2)}) collective-permute-start(bf16[4,16,16,128]{3,2,1,0:T(8,128)(2,1)S(1)} %get-tuple-element.13), channel_id=1, source_target_pairs={{0,11},{1,8},{2,9},{3,10},{4,15},{5,12},{6,13},{7,14},{8,3},{9,0},... | collective-permute-start | bytes 786440 | tf_op jit(solution)/shard_map/ppermute | solution.py:133
  75.2 18.9 %collective-permute-start.11 = (bf16[4,16,16,128]{3,2,1,0:T(8,128)(2,1)S(1)}, bf16[4,16,16,128]{3,2,1,0:T(8,128)(2,1)S(1)}, u32[]{:S(2)}, u32[]{:S(2)}) collective-permute-start(bf16[4,16,16,128]{3,2,1,0:T(8,128)(2,1)S(1)} %get-tuple-element.12), channel_id=1, source_target_pairs={{0,12},{1,13},{2,14},{3,15},{4,0},{5,1},{6,2},{7,3},{8,4},{9,5},{1... | collective-permute-start | bytes 786440 | tf_op jit(solution)/shard_map/ppermute | solution.py:133
  77.3 18.2 %collective-permute-start.12 = (bf16[4,16,16,128]{3,2,1,0:T(8,128)(2,1)S(1)}, bf16[4,16,16,128]{3,2,1,0:T(8,128)(2,1)S(1)}, u32[]{:S(2)}, u32[]{:S(2)}) collective-permute-start(bf16[4,16,16,128]{3,2,1,0:T(8,128)(2,1)S(1)} %get-tuple-element.11), channel_id=1, source_target_pairs={{0,13},{1,14},{2,15},{3,12},{4,1},{5,2},{6,3},{7,0},{8,5},{9,6},{1... | collective-permute-start | bytes 786440 | tf_op jit(solution)/shard_map/ppermute | solution.py:133
  79.2 27.7 %collective-permute-start.13 = (bf16[4,16,16,128]{3,2,1,0:T(8,128)(2,1)S(1)}, bf16[4,16,16,128]{3,2,1,0:T(8,128)(2,1)S(1)}, u32[]{:S(2)}, u32[]{:S(2)}) collective-permute-start(bf16[4,16,16,128]{3,2,1,0:T(8,128)(2,1)S(1)} %get-tuple-element.10), channel_id=1, source_target_pairs={{0,14},{1,15},{2,12},{3,13},{4,2},{5,3},{6,0},{7,1},{8,6},{9,7},{1... | collective-permute-start | bytes 786440 | tf_op jit(solution)/shard_map/ppermute | solution.py:133
  85.6 22.7 %collective-permute-start.14 = (bf16[4,16,16,128]{3,2,1,0:T(8,128)(2,1)S(1)}, bf16[4,16,16,128]{3,2,1,0:T(8,128)(2,1)S(1)}, u32[]{:S(2)}, u32[]{:S(2)}) collective-permute-start(bf16[4,16,16,128]{3,2,1,0:T(8,128)(2,1)S(1)} %get-tuple-element.9), channel_id=1, source_target_pairs={{0,15},{1,12},{2,13},{3,14},{4,3},{5,0},{6,1},{7,2},{8,7},{9,4},{1... | collective-permute-start | bytes 786440 | tf_op jit(solution)/shard_map/ppermute | solution.py:133
  87.0 23.6 %collective-permute-start.2 = (bf16[4,16,16,128]{3,2,1,0:T(8,128)(2,1)S(1)}, bf16[4,16,16,128]{3,2,1,0:T(8,128)(2,1)S(1)}, u32[]{:S(2)}, u32[]{:S(2)}) collective-permute-start(bf16[4,16,16,128]{3,2,1,0:T(8,128)(2,1)S(1)} %get-tuple-element.21), channel_id=1, source_target_pairs={{0,3},{1,0},{2,1},{3,2},{4,7},{5,4},{6,5},{7,6},{8,11},{9,8},{10,9... | collective-permute-start | bytes 786440 | tf_op jit(solution)/shard_map/ppermute | solution.py:133
  94.0 18.2 %collective-permute-start.3 = (bf16[4,16,16,128]{3,2,1,0:T(8,128)(2,1)S(1)}, bf16[4,16,16,128]{3,2,1,0:T(8,128)(2,1)S(1)}, u32[]{:S(2)}, u32[]{:S(2)}) collective-permute-start(bf16[4,16,16,128]{3,2,1,0:T(8,128)(2,1)S(1)} %get-tuple-element.20), channel_id=1, source_target_pairs={{0,4},{1,5},{2,6},{3,7},{4,8},{5,9},{6,10},{7,11},{8,12},{9,13},{1... | collective-permute-start | bytes 786440 | tf_op jit(solution)/shard_map/ppermute | solution.py:133
  95.5 35.6 %collective-permute-start.4 = (bf16[4,16,16,128]{3,2,1,0:T(8,128)(2,1)S(1)}, bf16[4,16,16,128]{3,2,1,0:T(8,128)(2,1)S(1)}, u32[]{:S(2)}, u32[]{:S(2)}) collective-permute-start(bf16[4,16,16,128]{3,2,1,0:T(8,128)(2,1)S(1)} %get-tuple-element.19), channel_id=1, source_target_pairs={{0,5},{1,6},{2,7},{3,4},{4,9},{5,10},{6,11},{7,8},{8,13},{9,14},{1... | collective-permute-start | bytes 786440 | tf_op jit(solution)/shard_map/ppermute | solution.py:133
  106.9 25.1 %collective-permute-start.5 = (bf16[4,16,16,128]{3,2,1,0:T(8,128)(2,1)}, bf16[4,16,16,128]{3,2,1,0:T(8,128)(2,1)}, u32[]{:S(2)}, u32[]{:S(2)}) collective-permute-start(bf16[4,16,16,128]{3,2,1,0:T(8,128)(2,1)} %get-tuple-element.18), channel_id=1, source_target_pairs={{0,6},{1,7},{2,4},{3,5},{4,10},{5,11},{6,8},{7,9},{8,14},{9,15},{1... | collective-permute-start | bytes 786440 | tf_op jit(solution)/shard_map/ppermute | solution.py:133
  108.3 23.7 %collective-permute-start.6 = (bf16[4,16,16,128]{3,2,1,0:T(8,128)(2,1)}, bf16[4,16,16,128]{3,2,1,0:T(8,128)(2,1)}, u32[]{:S(2)}, u32[]{:S(2)}) collective-permute-start(bf16[4,16,16,128]{3,2,1,0:T(8,128)(2,1)} %get-tuple-element.17), channel_id=1, source_target_pairs={{0,7},{1,4},{2,5},{3,6},{4,11},{5,8},{6,9},{7,10},{8,15},{9,12},{1... | collective-permute-start | bytes 786440 | tf_op jit(solution)/shard_map/ppermute | solution.py:133
  110.6 33.8 %collective-permute-start.7 = (bf16[4,16,16,128]{3,2,1,0:T(8,128)(2,1)}, bf16[4,16,16,128]{3,2,1,0:T(8,128)(2,1)}, u32[]{:S(2)}, u32[]{:S(2)}) collective-permute-start(bf16[4,16,16,128]{3,2,1,0:T(8,128)(2,1)} %get-tuple-element.16), channel_id=1, source_target_pairs={{0,8},{1,9},{2,10},{3,11},{4,12},{5,13},{6,14},{7,15},{8,0},{9,1},... | collective-permute-start | bytes 786440 | tf_op jit(solution)/shard_map/ppermute | solution.py:133
  112.2 0.7 copy-start.1
  112.9 31.4 %collective-permute-start.8 = (bf16[4,16,16,128]{3,2,1,0:T(8,128)(2,1)}, bf16[4,16,16,128]{3,2,1,0:T(8,128)(2,1)}, u32[]{:S(2)}, u32[]{:S(2)}) collective-permute-start(bf16[4,16,16,128]{3,2,1,0:T(8,128)(2,1)} %get-tuple-element.15), channel_id=1, source_target_pairs={{0,9},{1,10},{2,11},{3,8},{4,13},{5,14},{6,15},{7,12},{8,1},{9,2},... | collective-permute-start | bytes 786440 | tf_op jit(solution)/shard_map/ppermute | solution.py:133
  131.1 0.7 copy-start.3
  131.8 12.5 %collective-permute-start.9 = (bf16[4,16,16,128]{3,2,1,0:T(8,128)(2,1)}, bf16[4,16,16,128]{3,2,1,0:T(8,128)(2,1)}, u32[]{:S(2)}, u32[]{:S(2)}) collective-permute-start(bf16[4,16,16,128]{3,2,1,0:T(8,128)(2,1)} %get-tuple-element.14), channel_id=1, source_target_pairs={{0,10},{1,11},{2,8},{3,9},{4,14},{5,15},{6,12},{7,13},{8,2},{9,3},... | collective-permute-start | bytes 786440 | tf_op jit(solution)/shard_map/ppermute | solution.py:133
  144.3 1.0 copy-start.2
  145.3 0.9 copy-start.4
